TPU v7x, 32 devices: a whole 2x2x4 slice. The times are simulated.
32 devices in a mesh: dp: 2 (over x), tp: 4 (over z), ep: 4 (over y, core).
Axes of the slice: x: 2, y: 2, z: 4, core: 2. Of those that a mesh axis runs over, the one named last changes fastest.
Arguments:
- hidden: bfloat16 [512, 1536], P(('dp', 'ep')), parts along dimension 0
- seq_lens: int32 [512], P(('dp', 'ep')), parts along dimension 0
- rope_cos: float32 [512, 32], P(('dp', 'ep')), parts along dimension 0
- rope_sin: float32 [512, 32], P(('dp', 'ep')), parts along dimension 0
- ln1_scale: bfloat16 [1536], replicated
- ln1_bias: bfloat16 [1536], replicated
- w_qkv: bfloat16 [1536, 2560], P(None, 'tp')
- b_qkv: bfloat16 [2560], P('tp')
- w_out: bfloat16 [1536, 1536], P('tp')
- b_out: bfloat16 [1536], replicated
- k_cache: bfloat16 [512, 512, 8, 64], P(('dp', 'ep'), None, 'tp'), parts along dimension 0
- v_cache: bfloat16 [512, 512, 8, 64], P(('dp', 'ep'), None, 'tp'), parts along dimension 0
- ln2_scale: bfloat16 [1536], replicated
- ln2_bias: bfloat16 [1536], replicated
- w_router: bfloat16 [1536, 40], replicated
- expert_ids: int32 [512, 8], P(('dp', 'ep')), parts along dimension 0
- w_gate: bfloat16 [40, 1536, 512], P('ep', None, 'tp')
- w_up: bfloat16 [40, 1536, 512], P('ep', None, 'tp')
- w_down: bfloat16 [40, 512, 1536], P('ep', 'tp')
Outputs:
- output 1: bfloat16 [512, 1536], P(('dp', 'ep')), parts along dimension 0
- output 2: bfloat16 [512, 512, 8, 64], P(('dp', 'ep'), None, 'tp'), parts along dimension 0
- output 3: bfloat16 [512, 512, 8, 64], P(('dp', 'ep'), None, 'tp'), parts along dimension 0
There are 2 independent parts. A program takes and returns all parts, laid end to end along the dimension named above; an argument that names none is the same for every part.
All inputs are finite; a program needn't handle non-finite values.
Results may differ from a plain program's by a relative error of at most 0.01133.
Values are sent between devices in bfloat16 or wider.
A program may use at most 1 GiB of HBM per device.

v0:
```python
import functools

import jax
import jax.numpy as jnp
from jax import lax
from jax.experimental import pallas as pl
from jax.experimental.pallas import tpu as pltpu
from jax.sharding import PartitionSpec as P

EPS = 1e-5
F32 = jnp.float32
BF16 = jnp.bfloat16
MESH = pl.DeviceIdType.MESH
VMEM_LIMIT = 66_400_000
MOE_LIMIT = 40_000_000
NT = (((1,), (1,)), ((), ()))
BB = 8
COLS = 3
PIECE = 16
AHEAD = 4
W_PARTS = 4


def normalize(vals_f32, ln_scale, ln_bias):
    row_mean = jnp.mean(vals_f32, axis=-1, keepdims=True)
    centered = vals_f32 - row_mean
    row_var = jnp.mean(centered * centered, axis=-1, keepdims=True)
    normed = centered * lax.rsqrt(row_var + EPS)
    return (normed * ln_scale + ln_bias).astype(BF16)


def row_of(vec_ref):
    return vec_ref[...].astype(F32)[None, :]


def attention_kernel(lens_hbm, hid_hbm, cos_hbm, sin_hbm, scale_hbm, bias_hbm, bqkv_hbm, wqkv_hbm, wout_hbm, k_hbm, v_hbm,
                     part_ref, ko_hbm, vo_hbm, lens_ref, hid_ref, cos_ref, sin_ref, scale_ref, bias_ref, bqkv_ref,
                     k_buf, v_buf, w_buf, wo_buf, q_buf, kn_buf, vn_buf, c_buf, in_sem, w_sem, wo_sem, k_sem, v_sem, ko_sem, vo_sem):
    n_rows = hid_ref.shape[0]
    n_blocks = n_rows // BB
    s_max = k_buf.shape[2]
    smalls = ((hid_hbm, hid_ref), (scale_hbm, scale_ref), (bias_hbm, bias_ref), (bqkv_hbm, bqkv_ref), (cos_hbm, cos_ref), (sin_hbm, sin_ref),
              (lens_hbm, lens_ref))
    small_copies = [pltpu.make_async_copy(src, dst, in_sem.at[i]) for i, (src, dst) in enumerate(smalls)]
    w_rows = w_buf.shape[0] // W_PARTS
    w_copies = [pltpu.make_async_copy(wqkv_hbm.at[pl.ds(i * w_rows, w_rows)], w_buf.at[pl.ds(i * w_rows, w_rows)], w_sem.at[i]) for i in range(W_PARTS)]
    wo_copy = pltpu.make_async_copy(wout_hbm, wo_buf, wo_sem)
    for copy in small_copies[:3] + w_copies + small_copies[3:]:
        copy.start()

    def fetch(i):
        rows = pl.ds(i * BB, BB)
        return (pltpu.make_async_copy(k_hbm.at[rows], k_buf.at[rows], k_sem.at[i]),
                pltpu.make_async_copy(v_hbm.at[rows], v_buf.at[rows], v_sem.at[i]))

    def flush(i):
        rows = pl.ds(i * BB, BB)
        return (pltpu.make_async_copy(k_buf.at[rows], ko_hbm.at[rows], ko_sem.at[i]),
                pltpu.make_async_copy(v_buf.at[rows], vo_hbm.at[rows], vo_sem.at[i]))

    def fetch_start(i):
        for copy in fetch(i):
            copy.start()

    for i in range(AHEAD):
        fetch_start(i)

    for copy in small_copies:
        copy.wait()
    normed = normalize(hid_ref[...].astype(F32), row_of(scale_ref), row_of(bias_ref))
    for copy in w_copies:
        copy.wait()
    fetch_start(AHEAD)
    qkv = jnp.dot(normed, w_buf[...], preferred_element_type=F32) + row_of(bqkv_ref)
    qkv = qkv.astype(BF16).astype(F32)
    qkv = jnp.concatenate([qkv, jnp.zeros((128 - n_rows, qkv.shape[1]), F32)], axis=0)
    feats = qkv.T
    cos_t = jnp.concatenate([cos_ref[...], jnp.zeros((32, 128 - n_rows), F32)], axis=1)
    sin_t = jnp.concatenate([sin_ref[...], jnp.zeros((32, 128 - n_rows), F32)], axis=1)

    def rotate(base):
        u, w = feats[base:base + 32], feats[base + 32:base + 64]
        return jnp.concatenate([u * cos_t - w * sin_t, w * cos_t + u * sin_t], axis=0).astype(BF16).astype(F32)

    zeros = jnp.zeros((64, 128), F32)
    for g in range(2):
        for j in range(3):
            q_rot = rotate(g * 320 + j * 64)
            both = jnp.concatenate([q_rot, zeros] if g == 0 else [zeros, q_rot], axis=0)
            q_buf[pl.ds(g * 3 + j, n_rows, stride=8), :] = both.T[:n_rows]
    for r in (6, 7):
        q_buf[pl.ds(r, n_rows, stride=8), :] = jnp.zeros((n_rows, 128), F32)
    k_new = jnp.concatenate([rotate(192), rotate(320 + 192)], axis=0)
    v_new = jnp.concatenate([feats[256:320], feats[320 + 256:320 + 320]], axis=0)
    for i in range(n_blocks):
        kn_buf[i] = k_new if i == 0 else pltpu.roll(k_new, 128 - i * BB, 1)
        vn_buf[i] = v_new if i == 0 else pltpu.roll(v_new, 128 - i * BB, 1)

    def block(i, carry):
        for copy in fetch(i):
            copy.wait()

        @pl.when(i + AHEAD + 1 < n_blocks)
        def _():
            fetch_start(i + AHEAD + 1)

        @pl.when(i == n_blocks - AHEAD - 1)
        def _():
            wo_copy.start()

        k_cols, v_cols = kn_buf[i], vn_buf[i]
        lane = lax.broadcasted_iota(jnp.int32, (128, 128), 1)
        position = lax.broadcasted_iota(jnp.int32, (8, s_max), 1)
        scores = []
        for j in range(BB):
            b = i * BB + j
            pos = lens_ref[b]
            first = pl.multiple_of((pos // 128) * 128, 128)
            hit = lane == pos - first
            window = pl.ds(first, 128)
            k_buf[b, :, window] = jnp.where(hit, k_cols[:, j:j + 1], k_buf[b, :, window].astype(F32)).astype(BF16)
            v_buf[b, :, window] = jnp.where(hit, v_cols[:, j:j + 1], v_buf[b, :, window].astype(F32)).astype(BF16)
            rows = pl.ds(pl.multiple_of(b * 8, 8), 8)
            one = jnp.dot(q_buf[rows, :].astype(BF16), k_buf[b], preferred_element_type=F32) * 0.125
            scores.append(jnp.where(position <= pos, one, -jnp.inf))
        scores = jnp.concatenate(scores, axis=0)
        top = jnp.max(scores, axis=1, keepdims=True)
        weights = jnp.exp(scores - top)
        probs = weights * (1.0 / jnp.sum(weights, axis=1, keepdims=True))
        for j in range(BB):
            b = i * BB + j
            rows = pl.ds(pl.multiple_of(b * 8, 8), 8)
            c_buf[rows, :] = lax.dot_general(probs[j * 8:j * 8 + 8].astype(BF16), v_buf[b], NT, preferred_element_type=F32)
        for copy in flush(i):
            copy.start()
        return carry

    lax.fori_loop(0, n_blocks, block, 0)
    heads = [c_buf[pl.ds(r, n_rows, stride=8), :] for r in range(6)]
    low = lax.broadcasted_iota(jnp.int32, (n_rows, 128), 1) < 64
    ctx = jnp.concatenate([
        jnp.where(low, heads[0], pltpu.roll(heads[1], 64, 1)),
        jnp.where(low, heads[2], heads[3]),
        jnp.where(low, pltpu.roll(heads[4], 64, 1), heads[5]),
    ], axis=1).astype(BF16)
    wo_copy.wait()
    part_ref[...] = jnp.dot(ctx, wo_buf[...], preferred_element_type=F32).astype(BF16)
    for i in range(n_blocks):
        for copy in flush(i):
            copy.wait()


def moe_kernel(hid_ref, part_ref, bout_ref, scale_ref, bias_ref, wr_ref, ids_ref, wg_hbm, wu_hbm, wd_hbm, out_ref,
               wgu, wd, wr, rs_recv, x1, h2, ids_buf, act, own_p, y_p, hi0, hi1, d0, d1, y_send, y_recv,
               t_f, t_b, z_recv, o_buf, wsem, ssem, rsem):
    z, ep = lax.axis_index("tp"), lax.axis_index("ep")
    n_rows, d_model = hid_ref.shape
    n_exp = wgu.shape[0]
    width = d_model // COLS
    z_peers = [lax.rem(z + dz, 4) for dz in (1, 2, 3)]
    y_peer = lax.rem(ep + 2, 4)
    partner = ep + 1 - 2 * lax.rem(ep, 2)
    diagonal = 3 - ep
    barrier = pltpu.get_barrier_semaphore()
    for peer in z_peers:
        pl.semaphore_signal(barrier, inc=1, device_id={"tp": peer}, device_id_type=MESH)
    for peer in (y_peer, partner, diagonal):
        pl.semaphore_signal(barrier, inc=1, device_id={"ep": peer}, device_id_type=MESH)

    loads = []
    for e in range(n_exp):
        loads.append(pltpu.make_async_copy(wg_hbm.at[e], wgu.at[e, :, 0:128], wsem.at[2 * e]))
        loads.append(pltpu.make_async_copy(wu_hbm.at[e], wgu.at[e, :, 128:256], wsem.at[2 * e + 1]))
    loads.append(pltpu.make_async_copy(wd_hbm, wd, wsem.at[2 * n_exp]))
    for load in loads:
        load.start()

    count = [0]

    def remote(src, dst, device):
        slot = count[0]
        count[0] += 1
        return pltpu.make_async_remote_copy(src_ref=src, dst_ref=dst, send_sem=ssem.at[slot], recv_sem=rsem.at[slot],
                                            device_id=device, device_id_type=MESH)

    def at(index, h, shard=0):
        return pl.ds(pl.multiple_of(shard * n_rows + index * 16 + h * PIECE, PIECE), PIECE)

    def rows_at(index):
        return pl.ds(pl.multiple_of(index * 16, 16), 16)

    def cols(n):
        return pl.ds(n * width, width)

    halves = range(16 // PIECE)
    z_order = [z] + [lax.rem(z + 4 - dz, 4) for dz in (1, 2, 3)]
    rs = [[remote(part_ref.at[at(z_peers[dz], h)], rs_recv.at[dz, pl.ds(h * PIECE, PIECE)], {"tp": z_peers[dz]}) for dz in range(3)] for h in halves]
    to_z = [[remote(h2.at[at(z, h)], h2.at[at(z, h)], {"tp": z_peers[dz]}) for dz in range(3)] for h in halves]
    to_p = [[remote(h2.at[at(z_order[k], h)], h2.at[at(z_order[k], h, 1)], {"ep": partner}) for k in range(4)] for h in halves]
    to_y = [[remote(h2.at[at(z_order[k], h)], h2.at[at(z_order[k], h, 2)], {"ep": y_peer}) for k in range(4)] for h in halves]
    y_to_p = [[remote(h2.at[at(z_order[k], h, 2)], h2.at[at(z_order[k], h, 3)], {"ep": partner}) for k in range(4)] for h in halves]
    mine = rows_at(z)
    to_ids = [remote(ids_ref, ids_buf.at[i + 1], {"ep": peer}) for i, peer in enumerate((partner, y_peer, diagonal))]
    chunks = range(COLS)
    to_d0 = [remote(hi0.at[n], d0.at[n], {"ep": partner}) for n in chunks]
    to_d = [remote(hi1.at[n], d1.at[n], {"ep": partner}) for n in chunks]
    to_yy = [remote(y_send.at[n], y_recv.at[n], {"ep": y_peer}) for n in chunks]
    to_zz = [[remote(t_b.at[n, rows_at(z_peers[dz])], z_recv.at[n, dz], {"tp": z_peers[dz]}) for dz in range(3)] for n in chunks]
    to_o = [[remote(o_buf.at[n, mine], o_buf.at[n, mine], {"tp": z_peers[dz]}) for dz in range(3)] for n in chunks]

    scale, bias, bout = row_of(scale_ref), row_of(bias_ref), row_of(bout_ref)
    ids_buf[0] = ids_ref[...]
    wr[...] = jnp.concatenate([wr_ref[...], jnp.zeros((128 - wr_ref.shape[0], d_model), BF16)], axis=0)
    pl.semaphore_wait(barrier, 6)

    for h in halves:
        for dz in range(3):
            rs[h][dz].start()
    for copy in to_ids:
        copy.start()
    for h in halves:
        for dz in range(3):
            rs[h][dz].wait_recv()
        got = pl.ds(h * PIECE, PIECE)
        total = part_ref[at(z, h), :].astype(F32) + rs_recv[0, got].astype(F32) + rs_recv[1, got].astype(F32) + rs_recv[2, got].astype(F32)
        row = (hid_ref[at(z, h), :].astype(F32) + total + bout).astype(BF16)
        x1[got, :] = row.astype(F32)
        h2[at(z, h), :] = normalize(row.astype(F32), scale, bias)
        for dz in range(3):
            to_z[h][dz].start()
        to_y[h][0].start()
        to_p[h][0].start()

    def relay(h, k):
        to_y[h][k].wait_recv()
        y_to_p[h][k].start()

    for h in halves:
        for dz in range(3):
            to_z[h][dz].wait_recv()
            to_y[h][dz + 1].start()
            to_p[h][dz + 1].start()
        relay(h, 0)

    def masks(shard):
        picks = ids_buf[shard]
        expert = lax.broadcasted_iota(jnp.int32, (128, n_rows), 0)
        hit = jnp.zeros((128, n_rows), F32)
        for k in range(picks.shape[0]):
            hit = jnp.where(expert == picks[k:k + 1, :], 1.0, hit)
        return hit.T

    def toks(shard):
        return h2[shard * n_rows:(shard + 1) * n_rows, :]

    def gates_of(shard):
        logits = lax.dot_general(toks(shard), wr[...], NT, preferred_element_type=F32)
        logits = jnp.where(masks(shard) > 0.5, logits, -jnp.inf)
        shifted = jnp.exp(logits - jnp.max(logits, axis=1, keepdims=True))
        gates = (shifted / jnp.sum(shifted, axis=1, keepdims=True)).astype(BF16).astype(F32)
        return pltpu.roll(gates, lax.rem(128 - ep * n_exp, 128), 1)

    def up(shard, gates, first, last):
        rows = toks(shard)
        for e in range(first, last):
            if shard == 0:
                loads[2 * e].wait()
                loads[2 * e + 1].wait()
            pre = jnp.dot(rows, wgu[e], preferred_element_type=F32)
            gate_pre, up_pre = pre[:, :128], pre[:, 128:]
            hidden = (gate_pre * jax.nn.sigmoid(gate_pre) * up_pre).astype(BF16).astype(F32)
            act[shard * n_rows:(shard + 1) * n_rows, e * 128:(e + 1) * 128] = (hidden * gates[:, e:e + 1]).astype(BF16)

    for copy in to_ids:
        copy.wait_recv()
    up(0, gates_of(0), 0, n_exp)
    for h in halves:
        for copy in to_p[h]:
            copy.wait_recv()
    up(1, gates_of(1), 0, n_exp)
    for h in halves:
        for k in (1, 2, 3):
            relay(h, k)
    up(2, gates_of(2), 0, n_exp)
    for h in halves:
        for copy in y_to_p[h]:
            copy.wait_recv()
    up(3, gates_of(3), 0, n_exp)
    loads[-1].wait()

    def reduce_pair(n):
        to_d[n].wait_recv()
        y_send[n] = (y_p[n] + d1[n].astype(F32)).astype(BF16)
        to_yy[n].start()

    for n in chunks:
        both = jnp.dot(act[128:256, :], wd[:, cols(n)], preferred_element_type=F32)
        y_p[n] = both[0:64]
        hi1[n] = both[64:128].astype(BF16)
        to_d[n].start()
        if n > 0:
            reduce_pair(n - 1)
        both = jnp.dot(act[0:128, :], wd[:, cols(n)], preferred_element_type=F32)
        own_p[n] = both[0:64]
        hi0[n] = both[64:128].astype(BF16)
        to_d0[n].start()
    reduce_pair(COLS - 1)
    for n in chunks:
        to_d0[n].wait_recv()
        to_yy[n].wait_recv()
        t = own_p[n] + d0[n].astype(F32) + y_recv[n].astype(F32)
        t_f[n] = t
        t_b[n] = t.astype(BF16)
        for copy in to_zz[n]:
            copy.start()
    for n in chunks:
        for copy in to_zz[n]:
            copy.wait_recv()
        moe = t_f[n, mine, :] + z_recv[n, 0].astype(F32) + z_recv[n, 1].astype(F32) + z_recv[n, 2].astype(F32)
        o_buf[n, mine, :] = (x1[:, cols(n)] + moe).astype(BF16)
        for copy in to_o[n]:
            copy.start()
    for n in chunks:
        for copy in to_o[n]:
            copy.wait_recv()
        out_ref[:, cols(n)] = o_buf[n]
    for group in rs + to_z + to_p + to_y + y_to_p + [to_ids, to_d0, to_d, to_yy] + to_zz + to_o:
        for copy in group:
            copy.wait_send()


N_SLOTS = (16 // PIECE) * 18 + 3 + 9 * COLS


def solution(mesh):
    token_rows = P(('dp', 'ep'), None)
    token_vec = P(('dp', 'ep'))
    cache_spec = P(('dp', 'ep'), None, 'tp', None)
    expert_in = P('ep', None, 'tp')
    expert_down = P('ep', 'tp', None)
    vm = pl.BlockSpec(memory_space=pltpu.VMEM)
    anyspace = pl.BlockSpec(memory_space=pl.ANY)

    def device_step(hidden, seq_lens, rope_cos, rope_sin, ln1_scale, ln1_bias, w_qkv, b_qkv, w_out, b_out, k_cache, v_cache, ln2_scale, ln2_bias, w_router, expert_ids, w_gate, w_up, w_down):
        n, d = hidden.shape
        _, s_max, groups, head = k_cache.shape
        feat = groups * head
        n_exp = w_gate.shape[0]
        k_in = k_cache.transpose(0, 2, 3, 1).reshape(n, feat, s_max)
        v_in = v_cache.transpose(0, 2, 3, 1).reshape(n, feat, s_max)
        part, k_out, v_out = pl.pallas_call(
            attention_kernel,
            out_shape=(pltpu.VMEM((n, d), BF16), jax.ShapeDtypeStruct(k_in.shape, BF16), jax.ShapeDtypeStruct(v_in.shape, BF16)),
            in_specs=[anyspace] * 11,
            out_specs=(vm, anyspace, anyspace),
            scratch_shapes=[
                pltpu.SMEM((n,), jnp.int32), pltpu.VMEM((n, d), BF16), pltpu.VMEM((32, n), F32), pltpu.VMEM((32, n), F32),
                pltpu.VMEM((d,), BF16), pltpu.VMEM((d,), BF16), pltpu.VMEM(b_qkv.shape, BF16),
                pltpu.VMEM(k_in.shape, BF16), pltpu.VMEM(v_in.shape, BF16), pltpu.VMEM(w_qkv.shape, BF16), pltpu.VMEM(w_out.shape, BF16),
                pltpu.VMEM((n * 8, 128), F32), pltpu.VMEM((n // BB, 128, 128), F32), pltpu.VMEM((n // BB, 128, 128), F32), pltpu.VMEM((n * 8, 128), F32),
                pltpu.SemaphoreType.DMA((7,)), pltpu.SemaphoreType.DMA((W_PARTS,)), pltpu.SemaphoreType.DMA, pltpu.SemaphoreType.DMA((n // BB,)), pltpu.SemaphoreType.DMA((n // BB,)),
                pltpu.SemaphoreType.DMA((n // BB,)), pltpu.SemaphoreType.DMA((n // BB,)),
            ],
            compiler_params=pltpu.CompilerParams(vmem_limit_bytes=VMEM_LIMIT),
            name="attention",
        )(seq_lens, hidden, rope_cos.T, rope_sin.T, ln1_scale, ln1_bias, b_qkv, w_qkv, w_out, k_in, v_in)
        part = pltpu.with_memory_space_constraint(part, pltpu.VMEM)
        in_hbm = lambda w: pltpu.with_memory_space_constraint(w, pltpu.HBM)
        rows = lambda r, t: pltpu.VMEM((r, d), t)
        cut = lambda r, t: pltpu.VMEM((COLS, r, d // COLS), t)
        hidden_out = pl.pallas_call(
            moe_kernel,
            out_shape=pltpu.VMEM((n, d), BF16),
            in_specs=[vm] * 7 + [anyspace] * 3,
            out_specs=vm,
            scratch_shapes=[
                pltpu.VMEM((n_exp, d, 256), BF16), pltpu.VMEM((n_exp * 128, d), BF16), rows(128, BF16),
                pltpu.VMEM((3, 16, d), BF16), rows(16, F32), rows(256, BF16), pltpu.VMEM((4, 8, n), jnp.int32), pltpu.VMEM((256, n_exp * 128), BF16),
                cut(64, F32), cut(64, F32), cut(64, BF16), cut(64, BF16), cut(64, BF16), cut(64, BF16), cut(64, BF16), cut(64, BF16),
                cut(64, F32), cut(64, BF16), pltpu.VMEM((COLS, 3, 16, d // COLS), BF16), cut(64, BF16),
                pltpu.SemaphoreType.DMA((2 * n_exp + 1,)), pltpu.SemaphoreType.DMA((N_SLOTS,)), pltpu.SemaphoreType.DMA((N_SLOTS,)),
            ],
            compiler_params=pltpu.CompilerParams(vmem_limit_bytes=MOE_LIMIT, collective_id=0, has_side_effects=True),
            name="moe",
        )(hidden, part, b_out, ln2_scale, ln2_bias, w_router.T, expert_ids.T, in_hbm(w_gate), in_hbm(w_up), in_hbm(w_down.reshape(n_exp * 128, d)))
        unfold = lambda c: c.reshape(n, groups, head, s_max).transpose(0, 3, 1, 2)
        return hidden_out, unfold(k_out), unfold(v_out)

    in_specs = (token_rows, token_vec, token_rows, token_rows, P(), P(), P(None, 'tp'), P('tp'), P('tp', None), P(), cache_spec, cache_spec, P(), P(), P(), token_rows, expert_in, expert_in, expert_down)
    return jax.shard_map(device_step, mesh=mesh, in_specs=in_specs, out_specs=(token_rows, cache_spec, cache_spec), check_vma=False)
```

profile of v0, /device:TPU:0, one launch (start us, length us, event | category | flops | bytes accessed | tf_op | source)
XLA Modules:
  0.0 56.3 jit_solution(12080530006860364005)
XLA Ops:
  0.6 0.0 copy-start
  0.6 0.0 copy-start.1
  0.7 0.0 copy-start.2
  0.7 0.0 copy-start.3
  0.7 0.0 copy-start.4
  0.7 0.0 copy-start.5
  0.7 12.9 %attention.1 = (bf16[64,1536]{1,0:T(8,128)(2,1)S(1)}, bf16[64,128,512]{2,1,0:T(8,128)(2,1)}, bf16[64,128,512]{2,1,0:T(8,128)(2,1)}) custom-call(s32[64]{0:T(128)} %lens_hbm.1, bf16[64,1536]{1,0:T(8,128)(2,1)} %hid_ref.1, f32[32,64]{1,0:T(8,128)} %bitcast.22, f32[32,64]{1,0:T(8,128)} %bitcast.23, bf16[1536]{0:T(1024)(128)(2,1)} %scale_hbm.1, ...), custom_call_target="tpu_custom_call" | custom-call | tf_op jit(solution)/shard_map/attention/pallas_call | solution.py:351
  13.6 0.0 copy-done
  13.6 0.0 copy-done.1
  13.6 0.0 copy-done.2
  13.6 0.0 copy-done.3
  13.6 0.0 copy-done.4
  13.6 0.0 copy-done.5
  13.6 42.0 %moe.1 = bf16[64,1536]{1,0:T(8,128)(2,1)S(1)} custom-call(bf16[64,1536]{1,0:T(8,128)(2,1)S(1)} %copy-done, bf16[64,1536]{1,0:T(8,128)(2,1)S(1)} %get-tuple-element.6.part_ref, bf16[1536]{0:T(1024)(128)(2,1)S(1)} %copy-done.2, bf16[1536]{0:T(1024)(128)(2,1)S(1)} %copy-done.3, bf16[1536]{0:T(1024)(128)(2,1)S(1)} %copy-done.4, bf16[40,1536]{1,0:T(8,128)(2,1)S(1)} %bitcast.17, ...), custom_call_target="tpu_custom_call" | custom-call | tf_op jit(solution)/shard_map/moe/pallas_call | solution.py:371
  55.6 0.7 %copy.23 = bf16[64,1536]{1,0:T(8,128)(2,1)} copy(bf16[64,1536]{1,0:T(8,128)(2,1)S(1)} %moe.1) | data formatting | bytes 393216
Async XLA Ops:
  0.6 12.9 %copy-start = (bf16[64,1536]{1,0:T(8,128)(2,1)S(1)}, bf16[64,1536]{1,0:T(8,128)(2,1)}, u32[]{:S(2)}) copy-start(bf16[64,1536]{1,0:T(8,128)(2,1)} %hid_ref.1) | copy-start | bytes 589828
  0.6 12.9 %copy-start.1 = (bf16[1536,40]{0,1:T(8,128)(2,1)S(1)}, bf16[1536,40]{0,1:T(8,128)(2,1)}, u32[]{:S(2)}) copy-start(bf16[1536,40]{0,1:T(8,128)(2,1)} %param.33) | copy-start | bytes 368644
  0.7 12.9 %copy-start.2 = (bf16[1536]{0:T(1024)(128)(2,1)S(1)}, bf16[1536]{0:T(1024)(128)(2,1)}, u32[]{:S(2)}) copy-start(bf16[1536]{0:T(1024)(128)(2,1)} %bout_ref.1) | copy-start | bytes 9220
  0.7 12.9 %copy-start.3 = (bf16[1536]{0:T(1024)(128)(2,1)S(1)}, bf16[1536]{0:T(1024)(128)(2,1)}, u32[]{:S(2)}) copy-start(bf16[1536]{0:T(1024)(128)(2,1)} %scale_ref.1) | copy-start | bytes 9220
  0.7 12.9 %copy-start.4 = (bf16[1536]{0:T(1024)(128)(2,1)S(1)}, bf16[1536]{0:T(1024)(128)(2,1)}, u32[]{:S(2)}) copy-start(bf16[1536]{0:T(1024)(128)(2,1)} %bias_ref.1) | copy-start | bytes 9220
  0.7 12.9 %copy-start.5 = (s32[64,8]{0,1:T(8,128)S(1)}, s32[64,8]{0,1:T(8,128)}, u32[]{:S(2)}) copy-start(s32[64,8]{0,1:T(8,128)} %param.34) | copy-start | bytes 6148
where the time goes:
time: 56.5 us; the launch traced here: 56.3 us
  Pallas kernels  54.8 us (97%)
  between operations  0.75 us (1%)
  local copies, waits for them, and re-layouts  0.7 us (1%)
    pallas_call x1, Pallas kernels, device_step(): pl.pallas_call(moe_kernel, out_shape=pltpu.VMEM((n, d), BF16), in_specs=[...  42 us
    pallas_call x1, Pallas kernels, device_step(): pl.pallas_call(attention_kernel, out_shape=(pltpu.VMEM((n, d), BF16), jax...  12.9 us

commit v1 on v0

--- a/solution.py
+++ b/solution.py
@@ -17,7 +17,7 @@
 BB = 8
 COLS = 3
 PIECE = 16
-AHEAD = 4
+AHEAD = 6
 W_PARTS = 4
 
 

time: 56.5 us -> 57.3 us (1.014)
  Pallas kernels: 54.8 us -> 55.6 us
    pallas_call x1, Pallas kernels: 12.9 us -> 13.7 us  [device_step(): pl.pallas_call(attention_kernel, out_shape=(pltpu.VMEM((n, d), BF16), jax...]
where the time goes in v1:
time: 57.3 us; the launch traced here: 57.1 us
  Pallas kernels  55.6 us (97%)
  between operations  0.75 us (1%)
  local copies, waits for them, and re-layouts  0.7 us (1%)
    pallas_call x1, Pallas kernels, device_step(): pl.pallas_call(moe_kernel, out_shape=pltpu.VMEM((n, d), BF16), in_specs=[...  42 us
    pallas_call x1, Pallas kernels, device_step(): pl.pallas_call(attention_kernel, out_shape=(pltpu.VMEM((n, d), BF16), jax...  13.7 us

profile of v1, /device:TPU:0, one launch (start us, length us, event | category | flops | bytes accessed | tf_op | source)
XLA Modules:
  0.0 57.1 jit_solution(8845789071411520634)
XLA Ops:
  0.6 0.0 copy-start
  0.6 0.0 copy-start.1
  0.7 0.0 copy-start.2
  0.7 0.0 copy-start.3
  0.7 0.0 copy-start.4
  0.7 0.0 copy-start.5
  0.7 13.7 %attention.1 = (bf16[64,1536]{1,0:T(8,128)(2,1)S(1)}, bf16[64,128,512]{2,1,0:T(8,128)(2,1)}, bf16[64,128,512]{2,1,0:T(8,128)(2,1)}) custom-call(s32[64]{0:T(128)} %lens_hbm.1, bf16[64,1536]{1,0:T(8,128)(2,1)} %hid_ref.1, f32[32,64]{1,0:T(8,128)} %bitcast.22, f32[32,64]{1,0:T(8,128)} %bitcast.23, bf16[1536]{0:T(1024)(128)(2,1)} %scale_hbm.1, ...), custom_call_target="tpu_custom_call" | custom-call | tf_op jit(solution)/shard_map/attention/pallas_call | solution.py:351
  14.4 0.0 copy-done
  14.4 0.0 copy-done.1
  14.4 0.0 copy-done.2
  14.4 0.0 copy-done.3
  14.4 0.0 copy-done.4
  14.4 0.0 copy-done.5
  14.4 42.0 %moe.1 = bf16[64,1536]{1,0:T(8,128)(2,1)S(1)} custom-call(bf16[64,1536]{1,0:T(8,128)(2,1)S(1)} %copy-done, bf16[64,1536]{1,0:T(8,128)(2,1)S(1)} %get-tuple-element.6.part_ref, bf16[1536]{0:T(1024)(128)(2,1)S(1)} %copy-done.2, bf16[1536]{0:T(1024)(128)(2,1)S(1)} %copy-done.3, bf16[1536]{0:T(1024)(128)(2,1)S(1)} %copy-done.4, bf16[40,1536]{1,0:T(8,128)(2,1)S(1)} %bitcast.17, ...), custom_call_target="tpu_custom_call" | custom-call | tf_op jit(solution)/shard_map/moe/pallas_call | solution.py:371
  56.4 0.7 %copy.23 = bf16[64,1536]{1,0:T(8,128)(2,1)} copy(bf16[64,1536]{1,0:T(8,128)(2,1)S(1)} %moe.1) | data formatting | bytes 393216
Async XLA Ops:
  0.6 13.7 %copy-start = (bf16[64,1536]{1,0:T(8,128)(2,1)S(1)}, bf16[64,1536]{1,0:T(8,128)(2,1)}, u32[]{:S(2)}) copy-start(bf16[64,1536]{1,0:T(8,128)(2,1)} %hid_ref.1) | copy-start | bytes 589828
  0.6 13.7 %copy-start.1 = (bf16[1536,40]{0,1:T(8,128)(2,1)S(1)}, bf16[1536,40]{0,1:T(8,128)(2,1)}, u32[]{:S(2)}) copy-start(bf16[1536,40]{0,1:T(8,128)(2,1)} %param.33) | copy-start | bytes 368644
  0.7 13.7 %copy-start.2 = (bf16[1536]{0:T(1024)(128)(2,1)S(1)}, bf16[1536]{0:T(1024)(128)(2,1)}, u32[]{:S(2)}) copy-start(bf16[1536]{0:T(1024)(128)(2,1)} %bout_ref.1) | copy-start | bytes 9220
  0.7 13.7 %copy-start.3 = (bf16[1536]{0:T(1024)(128)(2,1)S(1)}, bf16[1536]{0:T(1024)(128)(2,1)}, u32[]{:S(2)}) copy-start(bf16[1536]{0:T(1024)(128)(2,1)} %scale_ref.1) | copy-start | bytes 9220
  0.7 13.7 %copy-start.4 = (bf16[1536]{0:T(1024)(128)(2,1)S(1)}, bf16[1536]{0:T(1024)(128)(2,1)}, u32[]{:S(2)}) copy-start(bf16[1536]{0:T(1024)(128)(2,1)} %bias_ref.1) | copy-start | bytes 9220
  0.7 13.7 %copy-start.5 = (s32[64,8]{0,1:T(8,128)S(1)}, s32[64,8]{0,1:T(8,128)}, u32[]{:S(2)}) copy-start(s32[64,8]{0,1:T(8,128)} %param.34) | copy-start | bytes 6148

commit v2 on v0

--- a/solution.py
+++ b/solution.py
@@ -33,9 +33,9 @@
     return vec_ref[...].astype(F32)[None, :]
 
 
-def attention_kernel(lens_hbm, hid_hbm, cos_hbm, sin_hbm, scale_hbm, bias_hbm, bqkv_hbm, wqkv_hbm, wout_hbm, k_hbm, v_hbm,
-                     part_ref, ko_hbm, vo_hbm, lens_ref, hid_ref, cos_ref, sin_ref, scale_ref, bias_ref, bqkv_ref,
-                     k_buf, v_buf, w_buf, wo_buf, q_buf, kn_buf, vn_buf, c_buf, in_sem, w_sem, wo_sem, k_sem, v_sem, ko_sem, vo_sem):
+def attention_kernel(lens_hbm, hid_hbm, cos_hbm, sin_hbm, scale_hbm, bias_hbm, bqkv_hbm, wqkv_hbm, k_hbm, v_hbm,
+                     ctx_ref, ko_hbm, vo_hbm, lens_ref, hid_ref, cos_ref, sin_ref, scale_ref, bias_ref, bqkv_ref,
+                     k_buf, v_buf, w_buf, q_buf, kn_buf, vn_buf, c_buf, in_sem, w_sem, k_sem, v_sem, ko_sem, vo_sem):
     n_rows = hid_ref.shape[0]
     n_blocks = n_rows // BB
     s_max = k_buf.shape[2]
@@ -44,7 +44,6 @@
     small_copies = [pltpu.make_async_copy(src, dst, in_sem.at[i]) for i, (src, dst) in enumerate(smalls)]
     w_rows = w_buf.shape[0] // W_PARTS
     w_copies = [pltpu.make_async_copy(wqkv_hbm.at[pl.ds(i * w_rows, w_rows)], w_buf.at[pl.ds(i * w_rows, w_rows)], w_sem.at[i]) for i in range(W_PARTS)]
-    wo_copy = pltpu.make_async_copy(wout_hbm, wo_buf, wo_sem)
     for copy in small_copies[:3] + w_copies + small_copies[3:]:
         copy.start()
 
@@ -103,10 +102,6 @@
         @pl.when(i + AHEAD + 1 < n_blocks)
         def _():
             fetch_start(i + AHEAD + 1)
-
-        @pl.when(i == n_blocks - AHEAD - 1)
-        def _():
-            wo_copy.start()
 
         k_cols, v_cols = kn_buf[i], vn_buf[i]
         lane = lax.broadcasted_iota(jnp.int32, (128, 128), 1)
@@ -138,20 +133,18 @@
     lax.fori_loop(0, n_blocks, block, 0)
     heads = [c_buf[pl.ds(r, n_rows, stride=8), :] for r in range(6)]
     low = lax.broadcasted_iota(jnp.int32, (n_rows, 128), 1) < 64
-    ctx = jnp.concatenate([
+    ctx_ref[...] = jnp.concatenate([
         jnp.where(low, heads[0], pltpu.roll(heads[1], 64, 1)),
         jnp.where(low, heads[2], heads[3]),
         jnp.where(low, pltpu.roll(heads[4], 64, 1), heads[5]),
     ], axis=1).astype(BF16)
-    wo_copy.wait()
-    part_ref[...] = jnp.dot(ctx, wo_buf[...], preferred_element_type=F32).astype(BF16)
     for i in range(n_blocks):
         for copy in flush(i):
             copy.wait()
 
 
-def moe_kernel(hid_ref, part_ref, bout_ref, scale_ref, bias_ref, wr_ref, ids_ref, wg_hbm, wu_hbm, wd_hbm, out_ref,
-               wgu, wd, wr, rs_recv, x1, h2, ids_buf, act, own_p, y_p, hi0, hi1, d0, d1, y_send, y_recv,
+def moe_kernel(hid_ref, ctx_ref, bout_ref, scale_ref, bias_ref, wr_ref, ids_ref, wout_hbm, wg_hbm, wu_hbm, wd_hbm, out_ref,
+               wout, part_ref, wgu, wd, wr, rs_recv, x1, h2, ids_buf, act, own_p, y_p, hi0, hi1, d0, d1, y_send, y_recv,
                t_f, t_b, z_recv, o_buf, wsem, ssem, rsem):
     z, ep = lax.axis_index("tp"), lax.axis_index("ep")
     n_rows, d_model = hid_ref.shape
@@ -167,13 +160,17 @@
     for peer in (y_peer, partner, diagonal):
         pl.semaphore_signal(barrier, inc=1, device_id={"ep": peer}, device_id_type=MESH)
 
+    wout_copy = pltpu.make_async_copy(wout_hbm, wout, wsem.at[2 * n_exp + 1])
+    wout_copy.start()
     loads = []
     for e in range(n_exp):
         loads.append(pltpu.make_async_copy(wg_hbm.at[e], wgu.at[e, :, 0:128], wsem.at[2 * e]))
         loads.append(pltpu.make_async_copy(wu_hbm.at[e], wgu.at[e, :, 128:256], wsem.at[2 * e + 1]))
     loads.append(pltpu.make_async_copy(wd_hbm, wd, wsem.at[2 * n_exp]))
+    wout_copy.wait()
     for load in loads:
         load.start()
+    part_ref[...] = jnp.dot(ctx_ref[...], wout[...], preferred_element_type=F32).astype(BF16)
 
     count = [0]
 
@@ -348,41 +345,41 @@
         n_exp = w_gate.shape[0]
         k_in = k_cache.transpose(0, 2, 3, 1).reshape(n, feat, s_max)
         v_in = v_cache.transpose(0, 2, 3, 1).reshape(n, feat, s_max)
-        part, k_out, v_out = pl.pallas_call(
+        ctx, k_out, v_out = pl.pallas_call(
             attention_kernel,
-            out_shape=(pltpu.VMEM((n, d), BF16), jax.ShapeDtypeStruct(k_in.shape, BF16), jax.ShapeDtypeStruct(v_in.shape, BF16)),
-            in_specs=[anyspace] * 11,
+            out_shape=(pltpu.VMEM((n, 384), BF16), jax.ShapeDtypeStruct(k_in.shape, BF16), jax.ShapeDtypeStruct(v_in.shape, BF16)),
+            in_specs=[anyspace] * 10,
             out_specs=(vm, anyspace, anyspace),
             scratch_shapes=[
                 pltpu.SMEM((n,), jnp.int32), pltpu.VMEM((n, d), BF16), pltpu.VMEM((32, n), F32), pltpu.VMEM((32, n), F32),
                 pltpu.VMEM((d,), BF16), pltpu.VMEM((d,), BF16), pltpu.VMEM(b_qkv.shape, BF16),
-                pltpu.VMEM(k_in.shape, BF16), pltpu.VMEM(v_in.shape, BF16), pltpu.VMEM(w_qkv.shape, BF16), pltpu.VMEM(w_out.shape, BF16),
+                pltpu.VMEM(k_in.shape, BF16), pltpu.VMEM(v_in.shape, BF16), pltpu.VMEM(w_qkv.shape, BF16),
                 pltpu.VMEM((n * 8, 128), F32), pltpu.VMEM((n // BB, 128, 128), F32), pltpu.VMEM((n // BB, 128, 128), F32), pltpu.VMEM((n * 8, 128), F32),
-                pltpu.SemaphoreType.DMA((7,)), pltpu.SemaphoreType.DMA((W_PARTS,)), pltpu.SemaphoreType.DMA, pltpu.SemaphoreType.DMA((n // BB,)), pltpu.SemaphoreType.DMA((n // BB,)),
+                pltpu.SemaphoreType.DMA((7,)), pltpu.SemaphoreType.DMA((W_PARTS,)), pltpu.SemaphoreType.DMA((n // BB,)), pltpu.SemaphoreType.DMA((n // BB,)),
                 pltpu.SemaphoreType.DMA((n // BB,)), pltpu.SemaphoreType.DMA((n // BB,)),
             ],
             compiler_params=pltpu.CompilerParams(vmem_limit_bytes=VMEM_LIMIT),
             name="attention",
-        )(seq_lens, hidden, rope_cos.T, rope_sin.T, ln1_scale, ln1_bias, b_qkv, w_qkv, w_out, k_in, v_in)
-        part = pltpu.with_memory_space_constraint(part, pltpu.VMEM)
+        )(seq_lens, hidden, rope_cos.T, rope_sin.T, ln1_scale, ln1_bias, b_qkv, w_qkv, k_in, v_in)
+        ctx = pltpu.with_memory_space_constraint(ctx, pltpu.VMEM)
         in_hbm = lambda w: pltpu.with_memory_space_constraint(w, pltpu.HBM)
         rows = lambda r, t: pltpu.VMEM((r, d), t)
         cut = lambda r, t: pltpu.VMEM((COLS, r, d // COLS), t)
         hidden_out = pl.pallas_call(
             moe_kernel,
             out_shape=pltpu.VMEM((n, d), BF16),
-            in_specs=[vm] * 7 + [anyspace] * 3,
+            in_specs=[vm] * 7 + [anyspace] * 4,
             out_specs=vm,
             scratch_shapes=[
-                pltpu.VMEM((n_exp, d, 256), BF16), pltpu.VMEM((n_exp * 128, d), BF16), rows(128, BF16),
+                pltpu.VMEM(w_out.shape, BF16), rows(64, BF16), pltpu.VMEM((n_exp, d, 256), BF16), pltpu.VMEM((n_exp * 128, d), BF16), rows(128, BF16),
                 pltpu.VMEM((3, 16, d), BF16), rows(16, F32), rows(256, BF16), pltpu.VMEM((4, 8, n), jnp.int32), pltpu.VMEM((256, n_exp * 128), BF16),
                 cut(64, F32), cut(64, F32), cut(64, BF16), cut(64, BF16), cut(64, BF16), cut(64, BF16), cut(64, BF16), cut(64, BF16),
                 cut(64, F32), cut(64, BF16), pltpu.VMEM((COLS, 3, 16, d // COLS), BF16), cut(64, BF16),
-                pltpu.SemaphoreType.DMA((2 * n_exp + 1,)), pltpu.SemaphoreType.DMA((N_SLOTS,)), pltpu.SemaphoreType.DMA((N_SLOTS,)),
+                pltpu.SemaphoreType.DMA((2 * n_exp + 2,)), pltpu.SemaphoreType.DMA((N_SLOTS,)), pltpu.SemaphoreType.DMA((N_SLOTS,)),
             ],
             compiler_params=pltpu.CompilerParams(vmem_limit_bytes=MOE_LIMIT, collective_id=0, has_side_effects=True),
             name="moe",
-        )(hidden, part, b_out, ln2_scale, ln2_bias, w_router.T, expert_ids.T, in_hbm(w_gate), in_hbm(w_up), in_hbm(w_down.reshape(n_exp * 128, d)))
+        )(hidden, ctx, b_out, ln2_scale, ln2_bias, w_router.T, expert_ids.T, in_hbm(w_out), in_hbm(w_gate), in_hbm(w_up), in_hbm(w_down.reshape(n_exp * 128, d)))
         unfold = lambda c: c.reshape(n, groups, head, s_max).transpose(0, 3, 1, 2)
         return hidden_out, unfold(k_out), unfold(v_out)
 

time: 56.5 us -> 58.4 us (1.034)
  Pallas kernels: 54.8 us -> 56.7 us
    pallas_call x1, Pallas kernels: 42 us -> 43.9 us  [device_step(): pl.pallas_call(moe_kernel, out_shape=pltpu.VMEM((n, d), BF16), in_specs=[...]
where the time goes in v2:
time: 58.4 us; the launch traced here: 58.2 us
  Pallas kernels  56.7 us (97%)
  between operations  0.75 us (1%)
  local copies, waits for them, and re-layouts  0.7 us (1%)
    pallas_call x1, Pallas kernels, device_step(): pl.pallas_call(moe_kernel, out_shape=pltpu.VMEM((n, d), BF16), in_specs=[...  43.9 us
    pallas_call x1, Pallas kernels, device_step(): pl.pallas_call(attention_kernel, out_shape=(pltpu.VMEM((n, 384), BF16), j...  12.8 us

profile of v2, /device:TPU:0, one launch (start us, length us, event | category | flops | bytes accessed | tf_op | source)
XLA Modules:
  0.0 58.2 jit_solution(7762694025652172177)
XLA Ops:
  0.6 0.0 copy-start
  0.6 0.0 copy-start.1
  0.7 0.0 copy-start.2
  0.7 0.0 copy-start.3
  0.7 0.0 copy-start.4
  0.7 0.0 copy-start.5
  0.7 12.8 %attention.1 = (bf16[64,384]{1,0:T(8,128)(2,1)S(1)}, bf16[64,128,512]{2,1,0:T(8,128)(2,1)}, bf16[64,128,512]{2,1,0:T(8,128)(2,1)}) custom-call(s32[64]{0:T(128)} %lens_hbm.1, bf16[64,1536]{1,0:T(8,128)(2,1)} %hid_ref.1, f32[32,64]{1,0:T(8,128)} %bitcast.22, f32[32,64]{1,0:T(8,128)} %bitcast.23, bf16[1536]{0:T(1024)(128)(2,1)} %scale_hbm.1, ...), custom_call_target="tpu_custom_call" | custom-call | tf_op jit(solution)/shard_map/attention/pallas_call | solution.py:348
  13.6 0.0 copy-done
  13.6 0.0 copy-done.1
  13.6 0.0 copy-done.2
  13.6 0.0 copy-done.3
  13.6 0.0 copy-done.4
  13.6 0.0 copy-done.5
  13.6 43.9 %moe.1 = bf16[64,1536]{1,0:T(8,128)(2,1)S(1)} custom-call(bf16[64,1536]{1,0:T(8,128)(2,1)S(1)} %copy-done, bf16[64,384]{1,0:T(8,128)(2,1)S(1)} %get-tuple-element.6.ctx_ref, bf16[1536]{0:T(1024)(128)(2,1)S(1)} %copy-done.2, bf16[1536]{0:T(1024)(128)(2,1)S(1)} %copy-done.3, bf16[1536]{0:T(1024)(128)(2,1)S(1)} %copy-done.4, bf16[40,1536]{1,0:T(8,128)(2,1)S(1)} %bitcast.17, ...), custom_call_target="tpu_custom_call" | custom-call | tf_op jit(solution)/shard_map/moe/pallas_call | solution.py:368
  57.5 0.7 %copy.23 = bf16[64,1536]{1,0:T(8,128)(2,1)} copy(bf16[64,1536]{1,0:T(8,128)(2,1)S(1)} %moe.1) | data formatting | bytes 393216
Async XLA Ops:
  0.6 12.9 %copy-start = (bf16[64,1536]{1,0:T(8,128)(2,1)S(1)}, bf16[64,1536]{1,0:T(8,128)(2,1)}, u32[]{:S(2)}) copy-start(bf16[64,1536]{1,0:T(8,128)(2,1)} %hid_ref.1) | copy-start | bytes 589828
  0.6 12.9 %copy-start.1 = (bf16[1536,40]{0,1:T(8,128)(2,1)S(1)}, bf16[1536,40]{0,1:T(8,128)(2,1)}, u32[]{:S(2)}) copy-start(bf16[1536,40]{0,1:T(8,128)(2,1)} %param.33) | copy-start | bytes 368644
  0.7 12.9 %copy-start.2 = (bf16[1536]{0:T(1024)(128)(2,1)S(1)}, bf16[1536]{0:T(1024)(128)(2,1)}, u32[]{:S(2)}) copy-start(bf16[1536]{0:T(1024)(128)(2,1)} %bout_ref.1) | copy-start | bytes 9220
  0.7 12.9 %copy-start.3 = (bf16[1536]{0:T(1024)(128)(2,1)S(1)}, bf16[1536]{0:T(1024)(128)(2,1)}, u32[]{:S(2)}) copy-start(bf16[1536]{0:T(1024)(128)(2,1)} %scale_ref.1) | copy-start | bytes 9220
  0.7 12.9 %copy-start.4 = (bf16[1536]{0:T(1024)(128)(2,1)S(1)}, bf16[1536]{0:T(1024)(128)(2,1)}, u32[]{:S(2)}) copy-start(bf16[1536]{0:T(1024)(128)(2,1)} %bias_ref.1) | copy-start | bytes 9220
  0.7 12.9 %copy-start.5 = (s32[64,8]{0,1:T(8,128)S(1)}, s32[64,8]{0,1:T(8,128)}, u32[]{:S(2)}) copy-start(s32[64,8]{0,1:T(8,128)} %param.34) | copy-start | bytes 6148

commit v3 on v1

--- a/solution.py
+++ b/solution.py
@@ -17,7 +17,7 @@
 BB = 8
 COLS = 3
 PIECE = 16
-AHEAD = 6
+AHEAD = 5
 W_PARTS = 4
 
 

time: 57.3 us -> 57.1 us (level)
    pallas_call x1, Pallas kernels: 13.7 us -> 13.1 us  [device_step(): pl.pallas_call(attention_kernel, out_shape=(pltpu.VMEM((n, d), BF16), jax...]
where the time goes in v3:
time: 57.1 us; the launch traced here: 56.9 us
  Pallas kernels  55.5 us (97%)
  between operations  0.75 us (1%)
  local copies, waits for them, and re-layouts  0.7 us (1%)
    pallas_call x1, Pallas kernels, device_step(): pl.pallas_call(moe_kernel, out_shape=pltpu.VMEM((n, d), BF16), in_specs=[...  42.4 us
    pallas_call x1, Pallas kernels, device_step(): pl.pallas_call(attention_kernel, out_shape=(pltpu.VMEM((n, d), BF16), jax...  13.1 us

profile of v3, /device:TPU:0, one launch (start us, length us, event | category | flops | bytes accessed | tf_op | source)
XLA Modules:
  0.0 56.9 jit_solution(8523225027518688237)
XLA Ops:
  0.6 0.0 copy-start
  0.6 0.0 copy-start.1
  0.7 0.0 copy-start.2
  0.7 0.0 copy-start.3
  0.7 0.0 copy-start.4
  0.7 0.0 copy-start.5
  0.7 13.1 %attention.1 = (bf16[64,1536]{1,0:T(8,128)(2,1)S(1)}, bf16[64,128,512]{2,1,0:T(8,128)(2,1)}, bf16[64,128,512]{2,1,0:T(8,128)(2,1)}) custom-call(s32[64]{0:T(128)} %lens_hbm.1, bf16[64,1536]{1,0:T(8,128)(2,1)} %hid_ref.1, f32[32,64]{1,0:T(8,128)} %bitcast.22, f32[32,64]{1,0:T(8,128)} %bitcast.23, bf16[1536]{0:T(1024)(128)(2,1)} %scale_hbm.1, ...), custom_call_target="tpu_custom_call" | custom-call | tf_op jit(solution)/shard_map/attention/pallas_call | solution.py:351
  13.8 0.0 copy-done
  13.8 0.0 copy-done.1
  13.8 0.0 copy-done.2
  13.8 0.0 copy-done.3
  13.8 0.0 copy-done.4
  13.8 0.0 copy-done.5
  13.8 42.4 %moe.1 = bf16[64,1536]{1,0:T(8,128)(2,1)S(1)} custom-call(bf16[64,1536]{1,0:T(8,128)(2,1)S(1)} %copy-done, bf16[64,1536]{1,0:T(8,128)(2,1)S(1)} %get-tuple-element.6.part_ref, bf16[1536]{0:T(1024)(128)(2,1)S(1)} %copy-done.2, bf16[1536]{0:T(1024)(128)(2,1)S(1)} %copy-done.3, bf16[1536]{0:T(1024)(128)(2,1)S(1)} %copy-done.4, bf16[40,1536]{1,0:T(8,128)(2,1)S(1)} %bitcast.17, ...), custom_call_target="tpu_custom_call" | custom-call | tf_op jit(solution)/shard_map/moe/pallas_call | solution.py:371
  56.3 0.7 %copy.23 = bf16[64,1536]{1,0:T(8,128)(2,1)} copy(bf16[64,1536]{1,0:T(8,128)(2,1)S(1)} %moe.1) | data formatting | bytes 393216
Async XLA Ops:
  0.6 13.1 %copy-start = (bf16[64,1536]{1,0:T(8,128)(2,1)S(1)}, bf16[64,1536]{1,0:T(8,128)(2,1)}, u32[]{:S(2)}) copy-start(bf16[64,1536]{1,0:T(8,128)(2,1)} %hid_ref.1) | copy-start | bytes 589828
  0.6 13.1 %copy-start.1 = (bf16[1536,40]{0,1:T(8,128)(2,1)S(1)}, bf16[1536,40]{0,1:T(8,128)(2,1)}, u32[]{:S(2)}) copy-start(bf16[1536,40]{0,1:T(8,128)(2,1)} %param.33) | copy-start | bytes 368644
  0.7 13.1 %copy-start.2 = (bf16[1536]{0:T(1024)(128)(2,1)S(1)}, bf16[1536]{0:T(1024)(128)(2,1)}, u32[]{:S(2)}) copy-start(bf16[1536]{0:T(1024)(128)(2,1)} %bout_ref.1) | copy-start | bytes 9220
  0.7 13.1 %copy-start.3 = (bf16[1536]{0:T(1024)(128)(2,1)S(1)}, bf16[1536]{0:T(1024)(128)(2,1)}, u32[]{:S(2)}) copy-start(bf16[1536]{0:T(1024)(128)(2,1)} %scale_ref.1) | copy-start | bytes 9220
  0.7 13.1 %copy-start.4 = (bf16[1536]{0:T(1024)(128)(2,1)S(1)}, bf16[1536]{0:T(1024)(128)(2,1)}, u32[]{:S(2)}) copy-start(bf16[1536]{0:T(1024)(128)(2,1)} %bias_ref.1) | copy-start | bytes 9220
  0.7 13.1 %copy-start.5 = (s32[64,8]{0,1:T(8,128)S(1)}, s32[64,8]{0,1:T(8,128)}, u32[]{:S(2)}) copy-start(s32[64,8]{0,1:T(8,128)} %param.34) | copy-start | bytes 6148
